TPU v7x, 256 devices: a whole 4x4x8 slice. The times are simulated.
256 devices in a mesh: px: 8 (over z_hi, x), py: 32 (over y, z_lo, core).
Axes of the slice: x: 4, y: 4, z: 8 (z_hi: 2, z_lo: 4; z = z_hi * 4 + z_lo), core: 2. Of those that a mesh axis runs over, the one named last changes fastest.
Arguments:
- populations: float32 [19, 2, 2048, 2048], P(None, None, ('py', 'px')), may hold values from 0.02 to 0.12
- pore: int32 [2, 2048, 2048], P(None, ('py', 'px')), may hold values 0 or 1
Outputs:
- flow: float32 [19, 2, 2048, 2048], P(None, None, 'py', 'px')
All inputs are finite; a program needn't handle non-finite values. No bound on the sum of `pore` on one device may be relied on, other than what follows from the above.
Results may differ from a plain program's by a relative error of at most 0.0001.
Values sent between devices are 32-bit elements; how exact they have to be, the bound alone decides.
A program may use at most 128 MiB of HBM per device.

v0:
```python
import jax
import jax.numpy as jnp
from jax import lax
from jax.sharding import PartitionSpec as P

STEPS = 2


lattice_velocity = [
    (0, 0, 0),
    (1, 0, 0),
    (-1, 0, 0),
    (0, 1, 0),
    (0, -1, 0),
    (0, 0, 1),
    (0, 0, -1),
    (1, 1, 0),
    (-1, -1, 0),
    (1, -1, 0),
    (-1, 1, 0),
    (1, 0, 1),
    (-1, 0, -1),
    (1, 0, -1),
    (-1, 0, 1),
    (0, 1, 1),
    (0, -1, -1),
    (0, 1, -1),
    (0, -1, 1),
]
lattice_weights = [1.0 / 3.0] + [1.0 / 18.0] * 6 + [1.0 / 36.0] * 12
opposite = [0, 2, 1, 4, 3, 6, 5, 8, 7, 10, 9, 12, 11, 14, 13, 16, 15, 18, 17]
relax_time = 0.8
body_force = 0.005


def cut_along(x, dim, peers):
    dims = x.shape
    parts = x.reshape(*dims[:dim], peers, dims[dim] // peers, *dims[dim + 1 :])
    return jnp.moveaxis(parts, dim, 0)


def cut_rows(length, count):
    unit = 8 if length >= 8 * count else 1
    return [length // unit * k // count * unit for k in range(1, count)]


def laid_out(parts, dim):
    dims = list(parts.shape[1:])
    dims[dim] *= parts.shape[0]
    return jnp.moveaxis(parts, 0, dim).reshape(dims)


def cut_exchange(x, axis, pieces, split_dim, concat_dim):
    parts = cut_along(x, split_dim, lax.axis_size(axis))
    split_at = max(range(1, max(2, parts.ndim - 1)), key=lambda d: parts.shape[d])
    gathered = []
    for slab in jnp.split(parts, cut_rows(parts.shape[split_at], pieces), axis=split_at):
        if slab.size:
            gathered.append(lax.all_to_all(slab, axis, split_axis=0, concat_axis=0, tiled=True))
    return laid_out(jnp.concatenate(gathered, axis=split_at), concat_dim)


def with_halo(cells, sides, width):
    for axis, dim in sides:
        count = lax.axis_size(axis)
        head = lax.slice_in_dim(cells, 0, width, axis=dim)
        tail = lax.slice_in_dim(cells, cells.shape[dim] - width, cells.shape[dim], axis=dim)
        cells = jnp.concatenate(
            [
                lax.ppermute(tail, axis, [(i, (i + 1) % count) for i in range(count)]),
                cells,
                lax.ppermute(head, axis, [((i + 1) % count, i) for i in range(count)]),
            ],
            axis=dim,
        )
    return cells


def moment(fields, column):
    total = jnp.zeros_like(fields[0])
    for slot in range(len(lattice_velocity)):
        vector = lattice_velocity[slot]
        if vector[column] != 0:
            total = total + float(vector[column]) * fields[slot]
    return total


def collide(fields, fluid):
    density = jnp.where(fluid > 0.5, jnp.sum(fields, axis=0), 1.0)
    vel_first = moment(fields, 0) / density
    vel_second = moment(fields, 1) / density
    vel_third = moment(fields, 2) / density + relax_time * body_force
    speed = vel_first * vel_first + vel_second * vel_second + vel_third * vel_third
    result = []
    for slot in range(len(lattice_velocity)):
        vector = lattice_velocity[slot]
        along = vector[0] * vel_first + vector[1] * vel_second + vector[2] * vel_third
        equil = (
            lattice_weights[slot]
            * density
            * (1.0 + 3.0 * along + 4.5 * along * along - 1.5 * speed)
        )
        result.append(fields[slot] - (fields[slot] - equil) / relax_time)
    return jnp.stack(result) * fluid[None]


def stream(post, fluid):
    height = post.shape[2]
    width = post.shape[3]
    result = []
    for slot in range(len(lattice_velocity)):
        vector = lattice_velocity[slot]
        rows_from = 1 - vector[1]
        cols_from = 1 - vector[0]
        source = post[
            slot, :, rows_from : height - 2 + rows_from, cols_from : width - 2 + cols_from
        ]
        source = jnp.roll(source, vector[2], axis=0)
        open_cell = fluid[:, rows_from : height - 2 + rows_from, cols_from : width - 2 + cols_from]
        open_cell = jnp.roll(open_cell, vector[2], axis=0)
        bounced = post[opposite[slot], :, 1:-1, 1:-1]
        result.append(jnp.where(open_cell > 0.5, source, bounced))
    return jnp.stack(result) * fluid[None, :, 1:-1, 1:-1]


def body(populations, pore):
    count = populations.shape[0]
    stacked = jnp.concatenate([populations, pore.astype(jnp.float32)[None]], axis=0)
    pencil = cut_exchange(stacked, "px", 2, 3, 2)
    fields = pencil[:count]
    padded = with_halo(pencil, (("px", 3), ("py", 2)), 2)
    region = padded[count]
    fields = padded[:count]
    for step in range(STEPS):
        post = collide(fields, region)
        fields = stream(post, region)
        region = region[:, 1:-1, 1:-1]
    return fields


def solution(mesh):
    return jax.shard_map(
        body,
        mesh=mesh,
        in_specs=(P(None, None, ("py", "px"), None), P(None, ("py", "px"), None)),
        out_specs=P(None, None, "py", "px"),
        check_vma=False,
    )
```

profile of v0, /device:TPU:7, one launch (start us, length us, event | category | flops | bytes accessed | tf_op | source)
XLA Modules:
  0.0 129.4 jit_solution(13115235130510524145)
XLA Ops:
  0.0 2.8 %copy.13 = f32[38,8,8,256]{3,2,1,0:T(8,128)S(1)} copy(f32[38,8,8,256]{3,1,2,0:T(8,128)} %bitcast.567) | data formatting | bytes 4980736
  2.9 0.3 maximum_bitcast_fusion
  3.3 1.3 %copy.4 = f32[8,8,2,8,256]{4,3,2,1,0:T(8,128)} copy(f32[8,8,2,8,256]{4,0,3,2,1:T(8,128)S(1)} %split.8) | data formatting | bytes 2097152 | tf_op jit(solution)/shard_map/split | solution.py:57
  4.6 10.8 %all-to-all-start = ((f32[8,8,2,8,256]{4,3,2,1,0:T(8,128)}), f32[8,8,2,8,256]{4,3,2,1,0:T(8,128)}, u32[]{:S(2)}, u32[]{:S(2)}) async-start(f32[8,8,2,8,256]{4,3,2,1,0:T(8,128)} %copy.4), calls=%async_computation | async-start | bytes 2097152 | tf_op jit(solution)/shard_map/all_to_all | solution.py:59
  15.4 0.1 split.9
  15.6 0.5 copy.5
  16.1 18.1 %all-to-all-done = f32[8,8,2,8,256]{4,3,2,1,0:T(8,128)} async-done(((f32[8,8,2,8,256]{4,3,2,1,0:T(8,128)}), f32[8,8,2,8,256]{4,3,2,1,0:T(8,128)}, u32[]{:S(2)}, u32[]{:S(2)}) %all-to-all-start) | async-done | bytes 1048608 | tf_op jit(solution)/shard_map/all_to_all | solution.py:59
  34.2 20.4 %all_to_all.10 = f32[8,12,2,8,256]{4,3,2,1,0:T(8,128)S(1)} all-to-all(f32[8,12,2,8,256]{4,3,2,1,0:T(8,128)S(1)} %copy.5), channel_id=1, replica_groups=mesh['px'=8,'py'=32] {'px'}, dimensions={0} | all-to-all | bytes 3145728 | tf_op jit(solution)/shard_map/all_to_all | solution.py:59
  54.6 1.6 %copy_bitcast_fusion = f32[20,2,64,256]{3,2,1,0:T(8,128)S(1)} fusion(f32[8,12,2,8,256]{4,3,2,1,0:T(8,128)S(1)} %all_to_all.10, f32[8,8,2,8,256]{4,3,2,1,0:T(8,128)} %all-to-all-done), kind=kLoop, calls=%fused_computation.4 | loop fusion | flops 655360 | bytes 5242880 | tf_op jit(solution)/shard_map/reshape | solution.py:50
  56.2 2.0 %fusion.341 = (f32[20,2,64,2]{3,2,1,0:T(8,128)}, f32[20,2,64,2]{3,2,1,0:T(8,128)}) fusion(f32[20,2,64,256]{3,2,1,0:T(8,128)S(1)} %copy_bitcast_fusion), kind=kLoop, calls=%fused_computation.555 | loop fusion | bytes 81920 | tf_op jit(solution)/shard_map/slice | solution.py:67
  58.2 1.8 %copy.8 = f32[20,2,64,2]{2,3,1,0:T(2,128)S(1)} copy(f32[20,2,64,2]{3,2,1,0:T(8,128)} %get-tuple-element.81) | data formatting | bytes 40960 | tf_op jit(solution)/shard_map/slice | solution.py:67
  59.9 7.5 %collective-permute-start = (f32[20,2,64,2]{2,3,1,0:T(2,128)S(1)}, f32[20,2,64,2]{2,3,1,0:T(2,128)S(1)}, u32[]{:S(2)}, u32[]{:S(2)}) collective-permute-start(f32[20,2,64,2]{2,3,1,0:T(2,128)S(1)} %copy.8), channel_id=1, source_target_pairs={{0,32},{32,64},{64,96},{96,128},{128,160},{160,192},{192,224},{224... | collective-permute-start | bytes 61448 | tf_op jit(solution)/shard_map/ppermute | solution.py:70
  67.5 1.8 %copy.9 = f32[20,2,64,2]{2,3,1,0:T(2,128)S(1)} copy(f32[20,2,64,2]{3,2,1,0:T(8,128)} %get-tuple-element.82) | data formatting | bytes 40960 | tf_op jit(solution)/shard_map/slice | solution.py:66
  69.3 8.9 %collective-permute-done = f32[20,2,64,2]{2,3,1,0:T(2,128)S(1)} collective-permute-done((f32[20,2,64,2]{2,3,1,0:T(2,128)S(1)}, f32[20,2,64,2]{2,3,1,0:T(2,128)S(1)}, u32[]{:S(2)}, u32[]{:S(2)}) %collective-permute-start) | collective-permute-done | bytes 20512 | tf_op jit(solution)/shard_map/ppermute | solution.py:70
  78.2 1.5 %copy.10 = f32[20,2,64,2]{3,2,1,0:T(8,128)} copy(f32[20,2,64,2]{2,3,1,0:T(2,128)S(1)} %collective-permute-done) | data formatting | bytes 40960 | tf_op jit(solution)/shard_map/ppermute | solution.py:70
  79.8 2.4 %collective-permute-done.1 = f32[20,2,64,2]{2,3,1,0:T(2,128)S(1)} collective-permute-done((f32[20,2,64,2]{2,3,1,0:T(2,128)S(1)}, f32[20,2,64,2]{2,3,1,0:T(2,128)S(1)}, u32[]{:S(2)}, u32[]{:S(2)}) %collective-permute-start.1) | collective-permute-done | bytes 20512 | tf_op jit(solution)/shard_map/ppermute | solution.py:72
  82.2 1.5 %copy.11 = f32[20,2,64,2]{3,2,1,0:T(8,128)} copy(f32[20,2,64,2]{2,3,1,0:T(2,128)S(1)} %collective-permute-done.1) | data formatting | bytes 40960 | tf_op jit(solution)/shard_map/ppermute | solution.py:72
  83.7 1.7 %pad_maximum_fusion.4 = (f32[20,2,2,260]{3,2,1,0:T(2,128)S(1)}, f32[20,2,2,260]{3,2,1,0:T(2,128)S(1)}) fusion(f32[20,2,64,2]{3,2,1,0:T(8,128)} %copy.11, f32[20,2,64,256]{3,2,1,0:T(8,128)S(1)} %copy_bitcast_fusion, f32[20,2,64,2]{3,2,1,0:T(8,128)} %copy.10), kind=kLoop, calls=%fused_computation.529 | loop fusion | flops 83200 | bytes 2828800 | tf_op jit(solution)/shard_map/slice | solution.py:67
  85.4 21.4 %collective-permute-start.2 = (f32[20,2,2,260]{3,2,1,0:T(2,128)S(1)}, f32[20,2,2,260]{3,2,1,0:T(2,128)S(1)}, u32[]{:S(2)}, u32[]{:S(2)}) collective-permute-start(f32[20,2,2,260]{3,2,1,0:T(2,128)S(1)} %get-tuple-element.39), channel_id=1, source_target_pairs={{0,1},{1,2},{2,3},{3,4},{4,5},{5,6},{6,7},{7,8},{8,9},{9,10},{10,1... | collective-permute-start | bytes 249608 | tf_op jit(solution)/shard_map/ppermute | solution.py:70
  106.8 1.9 %collective-permute-done.2 = f32[20,2,2,260]{3,2,1,0:T(2,128)S(1)} collective-permute-done((f32[20,2,2,260]{3,2,1,0:T(2,128)S(1)}, f32[20,2,2,260]{3,2,1,0:T(2,128)S(1)}, u32[]{:S(2)}, u32[]{:S(2)}) %collective-permute-start.2) | collective-permute-done | bytes 83232 | tf_op jit(solution)/shard_map/ppermute | solution.py:70
  108.7 2.4 %collective-permute-done.3 = f32[20,2,2,260]{3,2,1,0:T(2,128)S(1)} collective-permute-done((f32[20,2,2,260]{3,2,1,0:T(2,128)S(1)}, f32[20,2,2,260]{3,2,1,0:T(2,128)S(1)}, u32[]{:S(2)}, u32[]{:S(2)}) %collective-permute-start.3) | collective-permute-done | bytes 83232 | tf_op jit(solution)/shard_map/ppermute | solution.py:72
  111.1 1.7 %pad_maximum_fusion = f32[20,2,68,260]{3,2,1,0:T(8,128)S(1)} fusion(f32[20,2,2,260]{3,2,1,0:T(2,128)S(1)} %collective-permute-done.3, f32[20,2,64,2]{3,2,1,0:T(8,128)S(1)} %copy-done.1, f32[20,2,64,256]{3,2,1,0:T(8,128)S(1)} %copy_bitcast_fusion, f32[20,2,64,2]{3,2,1,0:T(8,128)S(1)} %copy-done, f32[20,2,2,260]{3,2,1,0:T(2,128)S(1)} %collective-permute-done.2), kind=kLoop, calls=%fused_computation | loop fusion | flops 2828800 | bytes 5657600 | tf_op jit(solution)/shard_map/concatenate | solution.py:68
  112.8 0.2 slice_reduce_fusion
  113.1 0.5 fusion.6
  113.7 0.1 fusion.20
  114.0 0.1 fusion.34
  114.2 0.1 fusion.48
  114.5 0.1 fusion.62
  115.0 0.1 fusion.90
  115.3 0.1 fusion.104
  115.6 0.1 slice_bitcast_fusion.35
  115.8 0.1 fusion.132
  116.0 0.3 broadcast_multiply_fusion.2
  116.4 0.5 fusion.340
  116.9 0.3 slice_bitcast_fusion.53
  117.6 0.2 fusion.315
  117.8 0.2 fusion.312
  118.1 0.2 fusion.309
  118.8 0.2 fusion.301
  119.2 0.2 fusion.295
  119.4 0.1 fusion.292
  119.9 0.1 fusion.288
  120.5 0.4 fusion.338
  120.9 0.5 fusion.140
  121.5 0.1 fusion.156
  121.8 0.1 fusion.172
  122.1 0.1 fusion.188
  122.4 0.1 fusion.204
  122.9 0.1 fusion.236
  123.1 0.1 fusion.252
  123.4 0.1 fusion.268
  123.7 0.4 fusion.284
  124.0 0.3 broadcast_multiply_fusion
  124.4 0.3 fusion.339
  124.8 0.2 slice_bitcast_fusion.63
  125.2 0.1 constant_dynamic-update-slice_fusion.17
  125.4 0.2 constant_dynamic-update-slice_fusion.16
  125.5 0.2 constant_dynamic-update-slice_fusion.15
  125.7 0.2 constant_dynamic-update-slice_fusion.14
  126.1 0.1 constant_dynamic-update-slice_fusion.11
  126.3 0.2 constant_dynamic-update-slice_fusion.10
  126.5 0.1 constant_dynamic-update-slice_fusion.9
  126.6 0.2 constant_dynamic-update-slice_fusion.8
  127.7 1.8 %broadcast_multiply_fusion.3 = f32[19,2,64,256]{3,2,1,0:T(8,128)} fusion(f32[19,2,64,256]{3,2,1,0:T(8,128)S(1)} %constant_dynamic-update-slice_fusion, f32[2,64,256]{2,1,0:T(8,128)S(1)} %slice.1176), kind=kLoop, calls=%fused_computation.8 | loop fusion | flops 622592 | bytes 5111808 | tf_op jit(solution)/shard_map/mul | solution.py:123
  (58 shorter events, 5.8 us)
Async XLA Ops:
  0.0 2.8 %copy-start.2 = (s32[2,8,2048]{2,1,0:T(8,128)S(1)}, s32[2,8,2048]{2,1,0:T(8,128)}, u32[]{:S(2)}) copy-start(s32[2,8,2048]{2,1,0:T(8,128)} %param.3) | copy-start | bytes 393220
  4.6 29.6 %all-to-all-start = ((f32[8,8,2,8,256]{4,3,2,1,0:T(8,128)}), f32[8,8,2,8,256]{4,3,2,1,0:T(8,128)}, u32[]{:S(2)}, u32[]{:S(2)}) async-start(f32[8,8,2,8,256]{4,3,2,1,0:T(8,128)} %copy.4), calls=%async_computation | async-start | bytes 2097152 | tf_op jit(solution)/shard_map/all_to_all | solution.py:59
  59.9 18.3 %collective-permute-start = (f32[20,2,64,2]{2,3,1,0:T(2,128)S(1)}, f32[20,2,64,2]{2,3,1,0:T(2,128)S(1)}, u32[]{:S(2)}, u32[]{:S(2)}) collective-permute-start(f32[20,2,64,2]{2,3,1,0:T(2,128)S(1)} %copy.8), channel_id=1, source_target_pairs={{0,32},{32,64},{64,96},{96,128},{128,160},{160,192},{192,224},{224... | collective-permute-start | bytes 61448 | tf_op jit(solution)/shard_map/ppermute | solution.py:70
  69.2 12.9 %collective-permute-start.1 = (f32[20,2,64,2]{2,3,1,0:T(2,128)S(1)}, f32[20,2,64,2]{2,3,1,0:T(2,128)S(1)}, u32[]{:S(2)}, u32[]{:S(2)}) collective-permute-start(f32[20,2,64,2]{2,3,1,0:T(2,128)S(1)} %copy.9), channel_id=1, source_target_pairs={{32,0},{64,32},{96,64},{128,96},{160,128},{192,160},{224,192},{0,2... | collective-permute-start | bytes 61448 | tf_op jit(solution)/shard_map/ppermute | solution.py:72
  83.7 27.4 %copy-start = (f32[20,2,64,2]{3,2,1,0:T(8,128)S(1)}, f32[20,2,64,2]{3,2,1,0:T(8,128)}, u32[]{:S(2)}) copy-start(f32[20,2,64,2]{3,2,1,0:T(8,128)} %copy.10) | copy-start | bytes 61444
  83.7 27.4 %copy-start.1 = (f32[20,2,64,2]{3,2,1,0:T(8,128)S(1)}, f32[20,2,64,2]{3,2,1,0:T(8,128)}, u32[]{:S(2)}) copy-start(f32[20,2,64,2]{3,2,1,0:T(8,128)} %copy.11) | copy-start | bytes 61444
  85.4 23.3 %collective-permute-start.2 = (f32[20,2,2,260]{3,2,1,0:T(2,128)S(1)}, f32[20,2,2,260]{3,2,1,0:T(2,128)S(1)}, u32[]{:S(2)}, u32[]{:S(2)}) collective-permute-start(f32[20,2,2,260]{3,2,1,0:T(2,128)S(1)} %get-tuple-element.39), channel_id=1, source_target_pairs={{0,1},{1,2},{2,3},{3,4},{4,5},{5,6},{6,7},{7,8},{8,9},{9,10},{10,1... | collective-permute-start | bytes 249608 | tf_op jit(solution)/shard_map/ppermute | solution.py:70
  106.8 4.3 %collective-permute-start.3 = (f32[20,2,2,260]{3,2,1,0:T(2,128)S(1)}, f32[20,2,2,260]{3,2,1,0:T(2,128)S(1)}, u32[]{:S(2)}, u32[]{:S(2)}) collective-permute-start(f32[20,2,2,260]{3,2,1,0:T(2,128)S(1)} %get-tuple-element.40), channel_id=1, source_target_pairs={{1,0},{2,1},{3,2},{4,3},{5,4},{6,5},{7,6},{8,7},{9,8},{10,9},{11,1... | collective-permute-start | bytes 249608 | tf_op jit(solution)/shard_map/ppermute | solution.py:72
where the time goes:
time: 130 us; the launch traced here: 129 us
  starting transfers between devices  39.8 us (31%)
  waiting for transfers between devices  33.7 us (26%)
  blocking collectives  20.4 us (16%)
  other arithmetic  19.5 us (15%)
  local copies, waits for them, and re-layouts  15.5 us (12%)
    ppermute x2, starting transfers between devices, with_halo(): lax.ppermute(tail, axis, [(i, (i + 1) % count) for i in range(count)])  28.9 us
    all_to_all x1, blocking collectives, cut_exchange(): lax.all_to_all(slab, axis, split_axis=0, concat_axis=0, tiled=True)  20.4 us
    all_to_all x1, waiting for transfers between devices, cut_exchange(): lax.all_to_all(slab, axis, split_axis=0, concat_axis=0, tiled=True)  18.1 us
    all_to_all x1, starting transfers between devices, cut_exchange(): lax.all_to_all(slab, axis, split_axis=0, concat_axis=0, tiled=True)  10.8 us
    ppermute x2, waiting for transfers between devices, with_halo(): lax.ppermute(tail, axis, [(i, (i + 1) % count) for i in range(count)])  10.8 us
    unnamed x69, other arithmetic  10.4 us
    ppermute x2, waiting for transfers between devices, with_halo(): lax.ppermute(head, axis, [((i + 1) % count, i) for i in range(count)])  4.8 us
    slice x2, local copies, waits for them, and re-layouts, with_halo(): lax.slice_in_dim(cells, cells.shape[dim] - width, cells.shape[dim], axis=...  3.72 us
  transfers between devices with their start and end apart: 5, of which 5 were waited for; matrix products, arithmetic and copies ran while one was open for 3% of the time, Pallas kernels for 0%

commit v1 on v0

v1 whole, which is shorter than its diff:
```python
import functools

import jax
import jax.numpy as jnp
from jax import lax
from jax.experimental import pallas as pl
from jax.experimental.pallas import tpu as pltpu
from jax.sharding import PartitionSpec as P

lattice_velocity = [
    (0, 0, 0),
    (1, 0, 0),
    (-1, 0, 0),
    (0, 1, 0),
    (0, -1, 0),
    (0, 0, 1),
    (0, 0, -1),
    (1, 1, 0),
    (-1, -1, 0),
    (1, -1, 0),
    (-1, 1, 0),
    (1, 0, 1),
    (-1, 0, -1),
    (1, 0, -1),
    (-1, 0, 1),
    (0, 1, 1),
    (0, -1, -1),
    (0, 1, -1),
    (0, -1, 1),
]
lattice_weights = [1.0 / 3.0] + [1.0 / 18.0] * 6 + [1.0 / 36.0] * 12
opposite = [0, 2, 1, 4, 3, 6, 5, 8, 7, 10, 9, 12, 11, 14, 13, 16, 15, 18, 17]
relax_time = 0.8
body_force = 0.005

Q = 19
NZ = 2
KZ = Q * NZ
ROWS = 8
LANES = 128
COLS = 256
GROUP = 8
NX = 4
MESH = pl.DeviceIdType.MESH
f32 = jnp.float32


def tree_sum(values):
    values = list(values)
    while len(values) > 1:
        values = [
            values[i] + values[i + 1] if i + 1 < len(values) else values[i]
            for i in range(0, len(values), 2)
        ]
    return values[0]


def collide(fields, fluid):
    mass = tree_sum(fields)
    inverse = 1.0 / jnp.where(fluid > 0.5, mass, 1.0)
    speeds = []
    for column in range(3):
        plus = tree_sum([fields[i] for i in range(Q) if lattice_velocity[i][column] > 0])
        minus = tree_sum([fields[i] for i in range(Q) if lattice_velocity[i][column] < 0])
        speeds.append((plus - minus) * inverse)
    speeds[2] = speeds[2] + relax_time * body_force
    square = speeds[0] * speeds[0] + speeds[1] * speeds[1] + speeds[2] * speeds[2]
    rest = 1.0 - 1.5 * square
    triple = [3.0 * s for s in speeds]
    keep = 1.0 - 1.0 / relax_time
    result = [None] * Q
    scaled = {w: mass * (w / relax_time) for w in sorted(set(lattice_weights))}
    result[0] = keep * fields[0] + scaled[lattice_weights[0]] * rest
    for slot in range(1, Q, 2):
        vector = lattice_velocity[slot]
        along = None
        for column in range(3):
            if vector[column]:
                if along is None:
                    along = triple[column] if vector[column] > 0 else -triple[column]
                else:
                    along = along + triple[column] if vector[column] > 0 else along - triple[column]
        weight = scaled[lattice_weights[slot]]
        even = weight * (rest + 0.5 * along * along)
        odd = weight * along
        other = opposite[slot]
        result[slot] = keep * fields[slot] + (even + odd)
        result[other] = keep * fields[other] + (even - odd)
    return result


def exchange_kernel(
    pop_ref, pore_ref, pen_ref, strip, voxel, relay, fold, halo, in_sem, give_sem, carry_sem,
    send_x, send_z, send_y, recv_y,
):
    px = lax.axis_index("px")
    py = lax.axis_index("py")
    count = lax.axis_size("py")
    zh = px // NX
    xx = px % NX
    partner = (1 - zh) * NX + xx
    up = lax.rem(py + 1, count)
    down = lax.rem(py + count - 1, count)

    def across(b):
        return zh * NX + lax.rem(xx + b, NX)

    barrier = pltpu.get_barrier_semaphore()
    for where in [(partner, py), (across(1), py), (across(2), py), (across(3), py), (px, up), (px, down)]:
        pl.semaphore_signal(barrier, inc=1, device_id=where, device_id_type=MESH)

    load_pop = pltpu.make_async_copy(pop_ref, strip.at[pl.ds(0, KZ)], in_sem.at[0])
    load_pore = pltpu.make_async_copy(pore_ref, voxel, in_sem.at[1])
    load_pop.start()
    load_pore.start()
    load_pore.wait()
    load_pop.wait()

    def collide_tile(j, carry):
        cols = pl.ds(pl.multiple_of(j * LANES, LANES), LANES)
        for z in range(NZ):
            fluid = voxel[z, :, cols].astype(f32)
            fields = [strip[i * NZ + z, :, cols] * fluid for i in range(Q)]
            post = collide(fields, fluid)
            for i in range(Q):
                strip[i * NZ + z, :, cols] = post[i]
        return carry

    width = strip.shape[2]
    lax.fori_loop(0, width // LANES, collide_tile, 0)

    lane = lax.broadcasted_iota(jnp.int32, (ROWS, LANES), 1)

    def pack_sides(p, carry):
        left = pl.ds(pl.multiple_of(lax.rem(p * COLS + width - LANES, width), LANES), LANES)
        right = pl.ds(pl.multiple_of(lax.rem(p * COLS + COLS, width), LANES), LANES)
        for tile in range(2):
            total = jnp.zeros((ROWS, LANES), f32)
            for k in range(tile * 32, min(KZ, tile * 32 + 32)):
                shift = 4 * (k % 32)
                side = jnp.where(lane < LANES // 2, strip[k, :, right], strip[k, :, left])
                if shift:
                    side = pltpu.roll(side, shift, 1)
                total = jnp.where(((lane - shift + 2) & (LANES - 1)) < 4, side, total)
            cols = pl.ds(pl.multiple_of(p * COLS + tile * LANES, LANES), LANES)
            strip[KZ, :, cols] = total
        return carry

    lax.fori_loop(0, GROUP, pack_sides, 0)

    def place(s):
        return pen_ref.at[:, pl.ds(pl.multiple_of(s * ROWS + ROWS, ROWS), ROWS), :]

    def piece(p):
        return strip.at[:, :, pl.ds(pl.multiple_of(p * COLS, COLS), COLS)]

    pl.semaphore_wait(barrier, 6)

    first = pltpu.make_async_remote_copy(
        src_ref=piece(partner), dst_ref=place(px), send_sem=send_z.at[0], recv_sem=give_sem.at[px],
        device_id=(partner, py), device_id_type=MESH)
    first.start()
    sends = [first]
    for b in (1, 3, 2):
        copy = pltpu.make_async_remote_copy(
            src_ref=piece((1 - zh) * NX + lax.rem(xx + b, NX)), dst_ref=relay.at[b - 1],
            send_sem=send_x.at[b - 1], recv_sem=carry_sem.at[b - 1],
            device_id=(across(b), py), device_id_type=MESH)
        copy.start()
        sends.append(copy)
    for b in (1, 3, 2):
        copy = pltpu.make_async_remote_copy(
            src_ref=piece(across(b)), dst_ref=place(px),
            send_sem=send_x.at[b + 2], recv_sem=give_sem.at[px],
            device_id=(across(b), py), device_id_type=MESH)
        copy.start()
        sends.append(copy)

    own = pl.ds(pl.multiple_of(px * COLS, COLS), COLS)
    mine = pl.ds(pl.multiple_of(px * ROWS + ROWS, ROWS), ROWS)

    def copy_own(k, carry):
        pen_ref[k, mine, :] = strip[k, :, own]
        return carry

    lax.fori_loop(0, KZ + 1, copy_own, 0)

    edge = lax.rem(xx + zh, NX)
    late = (edge == 2).astype(jnp.int32)
    for n, b in enumerate((1, 3 - late, 2 + late)):
        source = zh * NX + lax.rem(xx + NX - b, NX)
        arrival = pltpu.make_async_remote_copy(
            src_ref=relay.at[b - 1], dst_ref=relay.at[b - 1], send_sem=send_z.at[n + 1],
            recv_sem=carry_sem.at[b - 1], device_id=(partner, py), device_id_type=MESH)
        arrival.wait_recv()
        onward = pltpu.make_async_remote_copy(
            src_ref=relay.at[b - 1], dst_ref=place(source), send_sem=send_z.at[n + 1],
            recv_sem=give_sem.at[source], device_id=(partner, py), device_id_type=MESH)
        onward.start()
        sends.append(onward)

    def await_strip(s):
        @pl.when(px != s)
        def _():
            pltpu.make_async_remote_copy(
                src_ref=place(s), dst_ref=place(s), send_sem=send_z.at[0], recv_sem=give_sem.at[s],
                device_id=(partner, py), device_id_type=MESH).wait_recv()

    row = lax.broadcasted_iota(jnp.int32, (ROWS, COLS), 0)

    def pack_rows(side):
        block = pl.ds(GROUP * ROWS, ROWS) if side == 0 else pl.ds(ROWS, ROWS)
        for group in range(10):
            total = jnp.zeros((ROWS, COLS), f32)
            for j in range(4):
                k = group * 4 + j
                if k > KZ:
                    continue
                shift = (2 * j + (2 if side == 0 else 0)) % ROWS
                part = pen_ref[k, block, :]
                if shift:
                    part = pltpu.roll(part, shift, 0)
                total = jnp.where((row >> 1) == j, part, total)
            fold[side, group] = total

    ways = []
    for side, s in ((0, GROUP - 1), (1, 0)):
        await_strip(s)
        pack_rows(side)
        way = pltpu.make_async_remote_copy(
            src_ref=fold.at[side], dst_ref=halo.at[side], send_sem=send_y.at[side],
            recv_sem=recv_y.at[side], device_id=(px, up if side == 0 else down), device_id_type=MESH)
        way.start()
        ways.append(way)

    for side in range(2):
        ways[side].wait()
        block = pl.ds(0, ROWS) if side == 0 else pl.ds((GROUP + 1) * ROWS, ROWS)
        for k in range(KZ + 1):
            shift = (ROWS - 2 * (k % 4) - (2 if side == 0 else 0)) % ROWS
            part = halo[side, k // 4]
            if shift:
                part = pltpu.roll(part, shift, 0)
            pen_ref[k, block, :] = part

    for s in range(1, GROUP - 1):
        await_strip(s)
    for copy in sends:
        copy.wait_send()


def exchange(pop, pore):
    blocks = GROUP + 2
    return pl.pallas_call(
        exchange_kernel,
        out_shape=jax.ShapeDtypeStruct((KZ + 1, blocks * ROWS, COLS), f32),
        in_specs=[pl.BlockSpec(memory_space=pl.ANY)] * 2,
        out_specs=pl.BlockSpec(memory_space=pltpu.VMEM),
        scratch_shapes=[
            pltpu.VMEM((KZ + 1, ROWS, pop.shape[2]), f32),
            pltpu.VMEM(pore.shape, jnp.int32),
            pltpu.VMEM((3, KZ + 1, ROWS, COLS), f32),
            pltpu.VMEM((2, 10, ROWS, COLS), f32),
            pltpu.VMEM((2, 10, ROWS, COLS), f32),
            pltpu.SemaphoreType.DMA((2,)),
            pltpu.SemaphoreType.DMA((GROUP,)),
            pltpu.SemaphoreType.DMA((3,)),
            pltpu.SemaphoreType.DMA((6,)),
            pltpu.SemaphoreType.DMA((4,)),
            pltpu.SemaphoreType.DMA((2,)),
            pltpu.SemaphoreType.DMA((2,)),
        ],
        compiler_params=pltpu.CompilerParams(collective_id=0, has_side_effects=True),
        name="exchange",
    )(pop, pore)


def shifted(load, vector, lane, row):
    cx, cy = vector[0], vector[1]
    seam = LANES - 1 if cx > 0 else 0

    def along_x(dy):
        value = load(dy, 0)
        if cx:
            value = pltpu.roll(jnp.where(lane == seam, load(dy, -cx), value), cx % LANES, 1)
        return value

    value = along_x(0)
    if cy:
        edge = ROWS - 1 if cy > 0 else 0
        value = pltpu.roll(jnp.where(row == edge, along_x(-cy), value), cy % ROWS, 0)
    return value


def stream(load, load_fluid, z, lane, row):
    masks = {}
    fluid = load_fluid(z, 0, 0)
    result = []
    for slot in range(Q):
        vector = lattice_velocity[slot]
        if slot == 0:
            result.append(load(0, z, 0, 0) * fluid)
            continue
        plane = z ^ (vector[2] & 1)
        key = (vector[0], vector[1], plane)
        if key not in masks:
            masks[key] = shifted(functools.partial(load_fluid, plane), vector, lane, row) > 0.5
        source = shifted(functools.partial(load, slot, plane), vector, lane, row)
        result.append(jnp.where(masks[key], source, load(opposite[slot], z, 0, 0)) * fluid)
    return result, fluid


def steps_kernel(pen_ref, out_ref, side, open_ref, post, flow, out_sem):
    blocks = GROUP + 2
    lane = lax.broadcasted_iota(jnp.int32, (ROWS, LANES), 1)
    row = lax.broadcasted_iota(jnp.int32, (ROWS, LANES), 0)

    def rows_of(b):
        return pl.ds(pl.multiple_of(b * ROWS, ROWS), ROWS)

    def unfold(b, carry):
        rows = rows_of(b)
        for k in range(KZ):
            tile = k // 32
            part = pen_ref[KZ, rows, pl.ds(tile * LANES, LANES)]
            shift = -4 * (k % 32) % LANES
            side[k, rows, :] = pltpu.roll(part, shift, 1) if shift else part
        for z in range(NZ):
            mass = tree_sum([pen_ref[i * NZ + z, rows, :] for i in range(Q)])
            open_ref[z, rows, pl.ds(0, COLS)] = jnp.where(mass > 0.19, 1.0, 0.0)
            mass = tree_sum([side[i * NZ + z, rows, :] for i in range(Q)])
            open_ref[z, rows, pl.ds(COLS, LANES)] = jnp.where(mass > 0.19, 1.0, 0.0)
        return carry

    lax.fori_loop(0, blocks, unfold, 0)

    def near(b, dy):
        return rows_of(jnp.clip(b + dy, 0, blocks - 1)) if dy else rows_of(b)

    def first(b, carry):
        for tile in range(3):
            for z in range(NZ):

                def load(slot, plane, dy, dx):
                    t = (tile + dx) % 3
                    k = slot * NZ + plane
                    if t == 2:
                        return side[k, near(b, dy), :]
                    return pen_ref[k, near(b, dy), pl.ds(t * LANES, LANES)]

                def load_fluid(plane, dy, dx):
                    return open_ref[plane, near(b, dy), pl.ds((tile + dx) % 3 * LANES, LANES)]

                fields, fluid = stream(load, load_fluid, z, lane, row)
                for i, value in enumerate(collide(fields, fluid)):
                    post[i * NZ + z, rows_of(b), pl.ds(tile * LANES, LANES)] = value
        return carry

    lax.fori_loop(0, blocks, first, 0)

    def leave(b):
        return pltpu.make_async_copy(
            flow.at[:, pl.ds(pl.multiple_of((b - 1) * ROWS, ROWS), ROWS), :],
            out_ref.at[:, pl.ds(pl.multiple_of((b - 1) * ROWS, ROWS), ROWS), :],
            out_sem.at[b - 1])

    def second(b, carry):
        for tile in range(2):
            for z in range(NZ):

                def load(slot, plane, dy, dx):
                    return post[slot * NZ + plane, near(b, dy), pl.ds((tile + dx) % 3 * LANES, LANES)]

                def load_fluid(plane, dy, dx):
                    return open_ref[plane, near(b, dy), pl.ds((tile + dx) % 3 * LANES, LANES)]

                fields, _ = stream(load, load_fluid, z, lane, row)
                for i, value in enumerate(fields):
                    flow[i * NZ + z, pl.ds(pl.multiple_of((b - 1) * ROWS, ROWS), ROWS), pl.ds(tile * LANES, LANES)] = value
        leave(b).start()
        return carry

    lax.fori_loop(1, blocks - 1, second, 0)
    for b in range(1, blocks - 1):
        leave(b).wait()


def steps(pen):
    blocks = GROUP + 2
    return pl.pallas_call(
        steps_kernel,
        out_shape=jax.ShapeDtypeStruct((KZ, GROUP * ROWS, COLS), f32),
        in_specs=[pl.BlockSpec(memory_space=pltpu.VMEM)],
        out_specs=pl.BlockSpec(memory_space=pl.ANY),
        scratch_shapes=[
            pltpu.VMEM((KZ, blocks * ROWS, LANES), f32),
            pltpu.VMEM((NZ, blocks * ROWS, COLS + LANES), f32),
            pltpu.VMEM((KZ, blocks * ROWS, COLS + LANES), f32),
            pltpu.VMEM((KZ, GROUP * ROWS, COLS), f32),
            pltpu.SemaphoreType.DMA((GROUP,)),
        ],
        name="steps",
    )(pen)


def body(populations, pore):
    shape = populations.shape
    pen = exchange(populations.reshape(KZ, shape[2], shape[3]), pore)
    return steps(pen).reshape(Q, NZ, GROUP * ROWS, COLS)


def solution(mesh):
    return jax.shard_map(
        body,
        mesh=mesh,
        in_specs=(P(None, None, ("py", "px"), None), P(None, ("py", "px"), None)),
        out_specs=P(None, None, "py", "px"),
        check_vma=False,
    )
```

time: 130 us -> 78.4 us (0.60)
  the two profiles are of different devices: /device:TPU:7 before, /device:TPU:8 now
where the time goes in v1:
time: 78.4 us; the launch traced here: 78.3 us
  Pallas kernels  78.3 us (100%)
    pallas_call x1, Pallas kernels, exchange(): pl.pallas_call(exchange_kernel, out_shape=jax.ShapeDtypeStruct((KZ + 1, b...  69.9 us
    pallas_call x1, Pallas kernels, steps(): pl.pallas_call(steps_kernel, out_shape=jax.ShapeDtypeStruct((KZ, GROUP *...  8.37 us

profile of v1, /device:TPU:8, one launch (start us, length us, event | category | flops | bytes accessed | tf_op | source)
XLA Modules:
  0.0 78.3 jit_solution(10135396514325957848)
XLA Ops:
  0.0 69.9 %exchange.1.pen_ref = f32[39,80,256]{2,1,0:T(8,128)} custom-call(f32[38,8,2048]{2,1,0:T(8,128)} %bitcast.2, s32[2,8,2048]{2,1,0:T(8,128)} %pore_ref.1), custom_call_target="tpu_custom_call" | custom-call | tf_op jit(solution)/shard_map/exchange/pallas_call | solution.py:254
  69.9 8.4 %steps.1 = f32[38,64,256]{2,1,0:T(8,128)} custom-call(f32[39,80,256]{2,1,0:T(8,128)} %exchange.1.pen_ref), custom_call_target="tpu_custom_call" | custom-call | tf_op jit(solution)/shard_map/steps/pallas_call | solution.py:390

commit v2 on v0

v2 whole, which is shorter than its diff:
```python
import functools

import jax
import jax.numpy as jnp
from jax import lax
from jax.experimental import pallas as pl
from jax.experimental.pallas import tpu as pltpu
from jax.sharding import PartitionSpec as P

lattice_velocity = [
    (0, 0, 0),
    (1, 0, 0),
    (-1, 0, 0),
    (0, 1, 0),
    (0, -1, 0),
    (0, 0, 1),
    (0, 0, -1),
    (1, 1, 0),
    (-1, -1, 0),
    (1, -1, 0),
    (-1, 1, 0),
    (1, 0, 1),
    (-1, 0, -1),
    (1, 0, -1),
    (-1, 0, 1),
    (0, 1, 1),
    (0, -1, -1),
    (0, 1, -1),
    (0, -1, 1),
]
lattice_weights = [1.0 / 3.0] + [1.0 / 18.0] * 6 + [1.0 / 36.0] * 12
opposite = [0, 2, 1, 4, 3, 6, 5, 8, 7, 10, 9, 12, 11, 14, 13, 16, 15, 18, 17]
relax_time = 0.8
body_force = 0.005

Q = 19
NZ = 2
KZ = Q * NZ
ROWS = 8
LANES = 128
COLS = 256
GROUP = 8
NX = 4
MESH = pl.DeviceIdType.MESH
f32 = jnp.float32


def tree_sum(values):
    values = list(values)
    while len(values) > 1:
        values = [
            values[i] + values[i + 1] if i + 1 < len(values) else values[i]
            for i in range(0, len(values), 2)
        ]
    return values[0]


def collide(fields, fluid):
    mass = tree_sum(fields)
    inverse = 1.0 / jnp.where(fluid > 0.5, mass, 1.0)
    speeds = []
    for column in range(3):
        plus = tree_sum([fields[i] for i in range(Q) if lattice_velocity[i][column] > 0])
        minus = tree_sum([fields[i] for i in range(Q) if lattice_velocity[i][column] < 0])
        speeds.append((plus - minus) * inverse)
    speeds[2] = speeds[2] + relax_time * body_force
    square = speeds[0] * speeds[0] + speeds[1] * speeds[1] + speeds[2] * speeds[2]
    rest = 1.0 - 1.5 * square
    triple = [3.0 * s for s in speeds]
    keep = 1.0 - 1.0 / relax_time
    result = [None] * Q
    scaled = {w: mass * (w / relax_time) for w in sorted(set(lattice_weights))}
    result[0] = keep * fields[0] + scaled[lattice_weights[0]] * rest
    for slot in range(1, Q, 2):
        vector = lattice_velocity[slot]
        along = None
        for column in range(3):
            if vector[column]:
                if along is None:
                    along = triple[column] if vector[column] > 0 else -triple[column]
                else:
                    along = along + triple[column] if vector[column] > 0 else along - triple[column]
        weight = scaled[lattice_weights[slot]]
        even = weight * (rest + 0.5 * along * along)
        odd = weight * along
        other = opposite[slot]
        result[slot] = keep * fields[slot] + (even + odd)
        result[other] = keep * fields[other] + (even - odd)
    return result

BLOCKS = GROUP + 2
WIDE = COLS + LANES
WINDOW = 5
HALO_RANK = 4


def carried(px):
    late = (lax.rem(px % NX + px // NX, NX) == 2).astype(jnp.int32)
    return 1, 3 - late, 2 + late


def arrivals(px):
    xx = px % NX
    other = 1 - px // NX
    partner = other * NX + xx
    return (partner,) + tuple(other * NX + lax.rem(xx + NX - b, NX) for b in carried(partner))


def rows_of(b):
    return pl.ds(pl.multiple_of(b * ROWS, ROWS), ROWS)


def near(b, dy):
    return rows_of(jnp.clip(b + dy, 0, BLOCKS - 1)) if dy else rows_of(b)


def second_step(post_ref, open_ref, flow_ref, b, at, lane, row):
    for tile in range(2):

        def load(slot, plane, dy, dx):
            return post_ref[slot * NZ + plane, near(b, dy), pl.ds((tile + dx) % 3 * LANES, LANES)]

        def load_fluid(plane, dy, dx):
            return open_ref[plane, near(b, dy), pl.ds((tile + dx) % 3 * LANES, LANES)]

        for z in range(NZ):
            fields, _ = stream(load, load_fluid, z, lane, row)
            for i, value in enumerate(fields):
                flow_ref[i * NZ + z, at, pl.ds(tile * LANES, LANES)] = value


def shifted(load, vector, lane, row):
    cx, cy = vector[0], vector[1]
    seam = LANES - 1 if cx > 0 else 0

    def along_x(dy):
        value = load(dy, 0)
        if cx:
            value = pltpu.roll(jnp.where(lane == seam, load(dy, -cx), value), cx % LANES, 1)
        return value

    value = along_x(0)
    if cy:
        edge = ROWS - 1 if cy > 0 else 0
        value = pltpu.roll(jnp.where(row == edge, along_x(-cy), value), cy % ROWS, 0)
    return value


def stream(load, load_fluid, z, lane, row):
    masks = {}
    fluid = load_fluid(z, 0, 0)
    result = []
    for slot in range(Q):
        vector = lattice_velocity[slot]
        if slot == 0:
            result.append(load(0, z, 0, 0) * fluid)
            continue
        plane = z ^ (vector[2] & 1)
        key = (vector[0], vector[1], plane)
        if key not in masks:
            masks[key] = shifted(functools.partial(load_fluid, plane), vector, lane, row) > 0.5
        source = shifted(functools.partial(load, slot, plane), vector, lane, row)
        result.append(jnp.where(masks[key], source, load(opposite[slot], z, 0, 0)) * fluid)
    return result, fluid


def exchange_kernel(
    pop_ref, pore_ref, post_ref, open_ref, flow_ref, early, raw, voxel, strip, relay, fold, halo, pen, side,
    in_sem, give_sem, carry_sem, send_x, send_z, send_y, recv_y,
):
    px = lax.axis_index("px")
    py = lax.axis_index("py")
    count = lax.axis_size("py")
    zh = px // NX
    xx = px % NX
    partner = (1 - zh) * NX + xx
    up = lax.rem(py + 1, count)
    down = lax.rem(py + count - 1, count)

    def across(b):
        return zh * NX + lax.rem(xx + b, NX)

    barrier = pltpu.get_barrier_semaphore()
    for where in [(partner, py), (across(1), py), (across(2), py), (across(3), py), (px, up), (px, down)]:
        pl.semaphore_signal(barrier, inc=1, device_id=where, device_id_type=MESH)

    width = strip.shape[2]
    tiles = width // LANES

    def tile_at(t):
        return pl.ds(pl.multiple_of(lax.rem(t, tiles) * LANES, LANES), LANES)

    home = partner * 2 + tiles - 1
    loads = [
        pltpu.make_async_copy(pore_ref, voxel, in_sem.at[0]),
        pltpu.make_async_copy(pop_ref.at[:, :, tile_at(home)], early.at[:, :, pl.ds(0, LANES)], in_sem.at[1]),
        pltpu.make_async_copy(
            pop_ref.at[:, :, pl.ds(pl.multiple_of(partner * COLS, COLS), COLS)],
            early.at[:, :, pl.ds(LANES, COLS)], in_sem.at[2]),
        pltpu.make_async_copy(
            pop_ref.at[:, :, tile_at(home + 3)], early.at[:, :, pl.ds(LANES + COLS, LANES)], in_sem.at[3]),
        pltpu.make_async_copy(pop_ref, raw, in_sem.at[4]),
    ]
    for load in loads:
        load.start()

    lane = lax.broadcasted_iota(jnp.int32, (ROWS, LANES), 1)
    row = lax.broadcasted_iota(jnp.int32, (ROWS, LANES), 0)

    def collide_tile(source, cols, to):
        for z in range(NZ):
            fluid = voxel[z, :, to].astype(f32)
            fields = [source[i * NZ + z, :, cols] * fluid for i in range(Q)]
            for i, value in enumerate(collide(fields, fluid)):
                strip[i * NZ + z, :, to] = value

    def pack_sides(p):
        left = tile_at(p * 2 + tiles - 1)
        right = tile_at(p * 2 + 2)
        for tile in range(2):
            total = jnp.zeros((ROWS, LANES), f32)
            for k in range(tile * 32, min(KZ, tile * 32 + 32)):
                turn = 4 * (k % 32)
                part = jnp.where(lane < LANES // 2, strip[k, :, right], strip[k, :, left])
                if turn:
                    part = pltpu.roll(part, turn, 1)
                total = jnp.where(((lane - turn + 2) & (LANES - 1)) < 4, part, total)
            strip[KZ, :, tile_at(p * 2 + tile)] = total

    def early_tile(t, carry):
        collide_tile(early, pl.ds(pl.multiple_of(t * LANES, LANES), LANES), tile_at(home + t))
        return carry

    def late_tile(t, carry):
        collide_tile(raw, tile_at(home + t), tile_at(home + t))
        return carry

    def late_sides(n, carry):
        pack_sides(lax.rem(partner + n, GROUP))
        return carry

    def place(s):
        return pen.at[:, rows_of(s + 1), :]

    def piece(p):
        return strip.at[:, :, pl.ds(pl.multiple_of(p * COLS, COLS), COLS)]

    for load in loads[:4]:
        load.wait()
    lax.fori_loop(0, 4, early_tile, 0)
    pack_sides(partner)
    pl.semaphore_wait(barrier, 6)

    first = pltpu.make_async_remote_copy(
        src_ref=piece(partner), dst_ref=place(px), send_sem=send_z.at[0], recv_sem=give_sem.at[px],
        device_id=(partner, py), device_id_type=MESH)
    first.start()
    sends = [first]

    loads[4].wait()
    lax.fori_loop(4, tiles, late_tile, 0)
    lax.fori_loop(1, GROUP, late_sides, 0)

    order = (1, 3, 2)
    for n, b in enumerate(order):
        copy = pltpu.make_async_remote_copy(
            src_ref=piece((1 - zh) * NX + lax.rem(xx + b, NX)), dst_ref=relay.at[b - 1],
            send_sem=send_x.at[n], recv_sem=carry_sem.at[b - 1],
            device_id=(across(b), py), device_id_type=MESH)
        copy.start()
        sends.append(copy)
    for n, b in enumerate(order):
        copy = pltpu.make_async_remote_copy(
            src_ref=piece(across(b)), dst_ref=place(px),
            send_sem=send_x.at[n + 3], recv_sem=give_sem.at[px],
            device_id=(across(b), py), device_id_type=MESH)
        copy.start()
        sends.append(copy)

    own = pl.ds(pl.multiple_of(px * COLS, COLS), COLS)
    mine = rows_of(px + 1)

    def copy_own(k, carry):
        pen[k, mine, :] = strip[k, :, own]
        return carry

    lax.fori_loop(0, KZ + 1, copy_own, 0)

    for n, b in enumerate(carried(px)):
        source = zh * NX + lax.rem(xx + NX - b, NX)
        arrival = pltpu.make_async_remote_copy(
            src_ref=relay.at[b - 1], dst_ref=relay.at[b - 1], send_sem=send_z.at[n + 1],
            recv_sem=carry_sem.at[b - 1], device_id=(partner, py), device_id_type=MESH)
        arrival.wait_recv()
        onward = pltpu.make_async_remote_copy(
            src_ref=relay.at[b - 1], dst_ref=place(source), send_sem=send_z.at[n + 1],
            recv_sem=give_sem.at[source], device_id=(partner, py), device_id_type=MESH)
        onward.start()
        sends.append(onward)

    def await_strip(s):
        pltpu.make_async_remote_copy(
            src_ref=place(s), dst_ref=place(s), send_sem=send_z.at[0], recv_sem=give_sem.at[s],
            device_id=(partner, py), device_id_type=MESH).wait_recv()

    wide_row = lax.broadcasted_iota(jnp.int32, (ROWS, COLS), 0)

    def pack_rows(way):
        block = pl.ds(GROUP * ROWS, ROWS) if way == 0 else pl.ds(ROWS, ROWS)
        for group in range(10):
            total = jnp.zeros((ROWS, COLS), f32)
            for j in range(4):
                k = group * 4 + j
                if k > KZ:
                    continue
                turn = (2 * j + (2 if way == 0 else 0)) % ROWS
                part = pen[k, block, :]
                if turn:
                    part = pltpu.roll(part, turn, 0)
                total = jnp.where((wide_row >> 1) == j, part, total)
            fold[way, group] = total

    def unfold(b):
        rows = rows_of(b)
        for k in range(KZ):
            part = pen[KZ, rows, pl.ds(k // 32 * LANES, LANES)]
            turn = -4 * (k % 32) % LANES
            side[k, rows, :] = pltpu.roll(part, turn, 1) if turn else part
        for z in range(NZ):
            mass = tree_sum([pen[i * NZ + z, rows, :] for i in range(Q)])
            open_ref[z, rows, pl.ds(0, COLS)] = jnp.where(mass > 0.19, 1.0, 0.0)
            mass = tree_sum([side[i * NZ + z, rows, :] for i in range(Q)])
            open_ref[z, rows, pl.ds(COLS, LANES)] = jnp.where(mass > 0.19, 1.0, 0.0)

    def first_step(b):
        for tile in range(3):

            def load(slot, plane, dy, dx):
                t = (tile + dx) % 3
                k = slot * NZ + plane
                if t == 2:
                    return side[k, near(b, dy), :]
                return pen[k, near(b, dy), pl.ds(t * LANES, LANES)]

            def load_fluid(plane, dy, dx):
                return open_ref[plane, near(b, dy), pl.ds((tile + dx) % 3 * LANES, LANES)]

            for z in range(NZ):
                fields, fluid = stream(load, load_fluid, z, lane, row)
                for i, value in enumerate(collide(fields, fluid)):
                    post_ref[i * NZ + z, rows_of(b), pl.ds(tile * LANES, LANES)] = value

    coming = arrivals(px)
    last = coming[3]
    begin = jnp.clip(last - 2, 0, GROUP - WINDOW)

    def rank(b):
        s = b - 1
        late = jnp.where(s == last, 5, 3)
        for n in (2, 1, 0):
            late = jnp.where(s == coming[n], n + 1, late)
        late = jnp.where(s // NX == zh, 0, late)
        return jnp.where(jnp.logical_or(b <= 0, b >= BLOCKS - 1), HALO_RANK, late)

    def stage(n):
        def unfold_some(b, carry):
            @pl.when(rank(b) == n)
            def _():
                unfold(b)
            return carry

        def first_some(b, carry):
            @pl.when(jnp.maximum(jnp.maximum(rank(b - 1), rank(b)), rank(b + 1)) == n)
            def _():
                first_step(b)
            return carry

        lax.fori_loop(1, BLOCKS - 1, unfold_some, 0)
        lax.fori_loop(0, BLOCKS, first_some, 0)

    def half(n, carry):
        s = zh * NX + n

        @pl.when(s != px)
        def _():
            await_strip(s)
        return carry

    lax.fori_loop(0, NX, half, 0)
    stage(0)
    await_strip(coming[0])
    stage(1)
    await_strip(coming[1])
    stage(2)
    await_strip(coming[2])
    ways = []
    for way in range(2):
        pack_rows(way)
        copy = pltpu.make_async_remote_copy(
            src_ref=fold.at[way], dst_ref=halo.at[way], send_sem=send_y.at[way],
            recv_sem=recv_y.at[way], device_id=(px, up if way == 0 else down), device_id_type=MESH)
        copy.start()
        ways.append(copy)
    stage(3)
    for way in range(2):
        ways[way].wait()
        block = pl.ds(0, ROWS) if way == 0 else pl.ds((GROUP + 1) * ROWS, ROWS)
        for k in range(KZ + 1):
            turn = (ROWS - 2 * (k % 4) - (2 if way == 0 else 0)) % ROWS
            part = halo[way, k // 4]
            if turn:
                part = pltpu.roll(part, turn, 0)
            pen[k, block, :] = part
    unfold(0)
    unfold(BLOCKS - 1)
    stage(HALO_RANK)

    def second_come(n, carry):
        s = lax.rem(begin + WINDOW + n, GROUP)
        second_step(post_ref, open_ref, flow_ref, s + 1, rows_of(s), lane, row)
        return carry

    lax.fori_loop(0, GROUP - WINDOW, second_come, 0)
    await_strip(last)
    unfold(last + 1)

    def first_rest(b, carry):
        first_step(b)
        return carry

    lax.fori_loop(last, last + 3, first_rest, 0)
    for copy in sends:
        copy.wait_send()


def exchange(pop, pore):
    return pl.pallas_call(
        exchange_kernel,
        out_shape=[
            pltpu.VMEM((KZ, BLOCKS * ROWS, WIDE), f32),
            pltpu.VMEM((NZ, BLOCKS * ROWS, WIDE), f32),
            pltpu.VMEM((KZ, GROUP * ROWS, COLS), f32),
        ],
        in_specs=[pl.BlockSpec(memory_space=pltpu.HBM)] * 2,
        out_specs=[pl.BlockSpec(memory_space=pltpu.VMEM)] * 3,
        scratch_shapes=[
            pltpu.VMEM((KZ, ROWS, COLS + 2 * LANES), f32),
            pltpu.VMEM((KZ, ROWS, pop.shape[2]), f32),
            pltpu.VMEM(pore.shape, jnp.int32),
            pltpu.VMEM((KZ + 1, ROWS, pop.shape[2]), f32),
            pltpu.VMEM((3, KZ + 1, ROWS, COLS), f32),
            pltpu.VMEM((2, 10, ROWS, COLS), f32),
            pltpu.VMEM((2, 10, ROWS, COLS), f32),
            pltpu.VMEM((KZ + 1, BLOCKS * ROWS, COLS), f32),
            pltpu.VMEM((KZ, BLOCKS * ROWS, LANES), f32),
            pltpu.SemaphoreType.DMA((5,)),
            pltpu.SemaphoreType.DMA((GROUP,)),
            pltpu.SemaphoreType.DMA((3,)),
            pltpu.SemaphoreType.DMA((6,)),
            pltpu.SemaphoreType.DMA((4,)),
            pltpu.SemaphoreType.DMA((2,)),
            pltpu.SemaphoreType.DMA((2,)),
        ],
        compiler_params=pltpu.CompilerParams(collective_id=0, has_side_effects=True, vmem_limit_bytes=40 * 2**20),
        name="exchange",
    )(pltpu.with_memory_space_constraint(pop, pltpu.HBM), pltpu.with_memory_space_constraint(pore, pltpu.HBM))


def finish_kernel(post_ref, open_ref, flow_ref, out_ref, rest, out_sem):
    lane = lax.broadcasted_iota(jnp.int32, (ROWS, LANES), 1)
    row = lax.broadcasted_iota(jnp.int32, (ROWS, LANES), 0)
    last = arrivals(lax.axis_index("px"))[3]
    begin = jnp.clip(last - 2, 0, GROUP - WINDOW)

    def ready(n):
        s = lax.rem(begin + WINDOW + n, GROUP)
        return pltpu.make_async_copy(flow_ref.at[:, rows_of(s), :], out_ref.at[:, rows_of(s), :], out_sem.at[n + WINDOW])

    def fresh(n):
        return pltpu.make_async_copy(rest.at[:, rows_of(n), :], out_ref.at[:, rows_of(begin + n), :], out_sem.at[n])

    for n in range(GROUP - WINDOW):
        ready(n).start()

    def second_rest(n, carry):
        second_step(post_ref, open_ref, rest, begin + n + 1, rows_of(n), lane, row)
        fresh(n).start()
        return carry

    lax.fori_loop(0, WINDOW, second_rest, 0)
    for n in range(GROUP - WINDOW):
        ready(n).wait()
    for n in range(WINDOW):
        fresh(n).wait()


def finish(post, opened, flow):
    return pl.pallas_call(
        finish_kernel,
        out_shape=jax.ShapeDtypeStruct(flow.shape, f32),
        in_specs=[pl.BlockSpec(memory_space=pltpu.VMEM)] * 3,
        out_specs=pl.BlockSpec(memory_space=pl.ANY),
        scratch_shapes=[
            pltpu.VMEM((KZ, WINDOW * ROWS, COLS), f32),
            pltpu.SemaphoreType.DMA((GROUP,)),
        ],
        compiler_params=pltpu.CompilerParams(vmem_limit_bytes=24 * 2**20),
        name="finish",
    )(post, opened, flow)


def body(populations, pore):
    shape = populations.shape
    parts = exchange(populations.reshape(KZ, shape[2], shape[3]), pore)
    return finish(*parts).reshape(Q, NZ, GROUP * ROWS, COLS)


def solution(mesh):
    return jax.shard_map(
        body,
        mesh=mesh,
        in_specs=(P(None, None, ("py", "px"), None), P(None, ("py", "px"), None)),
        out_specs=P(None, None, "py", "px"),
        check_vma=False,
    )
```

time: 130 us -> 71.5 us (0.55)
  the two profiles are of different devices: /device:TPU:7 before, /device:TPU:30 now
where the time goes in v2:
time: 71.5 us; the launch traced here: 71.4 us
  Pallas kernels  71.4 us (100%)
    pallas_call x1, Pallas kernels, exchange(): pl.pallas_call(exchange_kernel, out_shape=[pltpu.VMEM((KZ, BLOCKS * ROWS,...  69.7 us
    pallas_call x1, Pallas kernels, finish(): pl.pallas_call(finish_kernel, out_shape=jax.ShapeDtypeStruct(flow.shape,...  1.7 us

profile of v2, /device:TPU:30, one launch (start us, length us, event | category | flops | bytes accessed | tf_op | source)
XLA Modules:
  0.0 71.4 jit_solution(8318322231644088006)
XLA Ops:
  0.0 69.7 %exchange.1 = (f32[38,80,384]{2,1,0:T(8,128)S(1)}, f32[2,80,384]{2,1,0:T(8,128)S(1)}, f32[38,64,256]{2,1,0:T(8,128)S(1)}) custom-call(f32[38,8,2048]{2,1,0:T(8,128)} %bitcast.2, s32[2,8,2048]{2,1,0:T(8,128)} %pore_ref.1), custom_call_target="tpu_custom_call" | custom-call | tf_op jit(solution)/shard_map/exchange/pallas_call | solution.py:437
  69.7 1.7 %finish.1 = f32[38,64,256]{2,1,0:T(8,128)} custom-call(f32[38,80,384]{2,1,0:T(8,128)S(1)} %get-tuple-element.8.post_ref, f32[2,80,384]{2,1,0:T(8,128)S(1)} %get-tuple-element.9.open_ref, f32[38,64,256]{2,1,0:T(8,128)S(1)} %get-tuple-element.10.flow_ref), custom_call_target="tpu_custom_call" | custom-call | tf_op jit(solution)/shard_map/finish/pallas_call | solution.py:498

commit v3 on v2

--- a/solution.py
+++ b/solution.py
@@ -88,15 +88,18 @@
         result[other] = keep * fields[other] + (even - odd)
     return result
 
-BLOCKS = GROUP + 2
+BLOCKS = GROUP + 1
 WIDE = COLS + LANES
 WINDOW = 5
+FRONT = 20
 HALO_RANK = 4
 
 
 def carried(px):
-    late = (lax.rem(px % NX + px // NX, NX) == 2).astype(jnp.int32)
-    return 1, 3 - late, 2 + late
+    edge = lax.rem(px % NX + px // NX, NX)
+    first = 1 + 2 * (edge == 3).astype(jnp.int32)
+    final = 2 + (edge == 2).astype(jnp.int32)
+    return first, 6 - first - final, final
 
 
 def arrivals(px):
@@ -111,7 +114,7 @@
 
 
 def near(b, dy):
-    return rows_of(jnp.clip(b + dy, 0, BLOCKS - 1)) if dy else rows_of(b)
+    return rows_of(lax.rem(b + dy + BLOCKS, BLOCKS)) if dy else rows_of(b)
 
 
 def second_step(post_ref, open_ref, flow_ref, b, at, lane, row):
@@ -269,6 +272,38 @@
             device_id=(across(b), py), device_id_type=MESH)
         copy.start()
         sends.append(copy)
+    own = pl.ds(pl.multiple_of(px * COLS, COLS), COLS)
+    mine = rows_of(px + 1)
+
+    def copy_own(k, carry):
+        pen[k, mine, :] = strip[k, :, own]
+        return carry
+
+    lax.fori_loop(0, KZ + 1, copy_own, 0)
+
+    def carry_on(n, b, parts):
+        source = zh * NX + lax.rem(xx + NX - b, NX)
+        pltpu.make_async_remote_copy(
+            src_ref=relay.at[b - 1], dst_ref=relay.at[b - 1], send_sem=send_z.at[n],
+            recv_sem=carry_sem.at[b - 1], device_id=(partner, py), device_id_type=MESH).wait_recv()
+        return [
+            pltpu.make_async_remote_copy(
+                src_ref=relay.at[b - 1, planes], dst_ref=pen.at[planes, rows_of(source + 1), :],
+                send_sem=send_z.at[n + m], recv_sem=give_sem.at[source if m == 0 else GROUP],
+                device_id=(partner, py), device_id_type=MESH)
+            for m, planes in enumerate(parts)
+        ]
+
+    whole = [pl.ds(0, KZ + 1)]
+    halves = [pl.ds(0, FRONT), pl.ds(FRONT, KZ + 1 - FRONT)]
+    turns = carried(px)
+    for n in range(2):
+        onward = carry_on(n + 1, turns[n], whole)
+        onward[0].start()
+        sends += onward
+    final = carry_on(3, turns[2], halves)
+    sends += final
+
     for n, b in enumerate(order):
         copy = pltpu.make_async_remote_copy(
             src_ref=piece(across(b)), dst_ref=place(px),
@@ -277,31 +312,17 @@
         copy.start()
         sends.append(copy)
 
-    own = pl.ds(pl.multiple_of(px * COLS, COLS), COLS)
-    mine = rows_of(px + 1)
-
-    def copy_own(k, carry):
-        pen[k, mine, :] = strip[k, :, own]
-        return carry
-
-    lax.fori_loop(0, KZ + 1, copy_own, 0)
-
-    for n, b in enumerate(carried(px)):
-        source = zh * NX + lax.rem(xx + NX - b, NX)
-        arrival = pltpu.make_async_remote_copy(
-            src_ref=relay.at[b - 1], dst_ref=relay.at[b - 1], send_sem=send_z.at[n + 1],
-            recv_sem=carry_sem.at[b - 1], device_id=(partner, py), device_id_type=MESH)
-        arrival.wait_recv()
-        onward = pltpu.make_async_remote_copy(
-            src_ref=relay.at[b - 1], dst_ref=place(source), send_sem=send_z.at[n + 1],
-            recv_sem=give_sem.at[source], device_id=(partner, py), device_id_type=MESH)
-        onward.start()
-        sends.append(onward)
-
     def await_strip(s):
         pltpu.make_async_remote_copy(
             src_ref=place(s), dst_ref=place(s), send_sem=send_z.at[0], recv_sem=give_sem.at[s],
             device_id=(partner, py), device_id_type=MESH).wait_recv()
+
+    def await_last(s):
+        for m, planes in enumerate(halves):
+            part = pen.at[planes, rows_of(s + 1), :]
+            pltpu.make_async_remote_copy(
+                src_ref=part, dst_ref=part, send_sem=send_z.at[0], recv_sem=give_sem.at[s if m == 0 else GROUP],
+                device_id=(partner, py), device_id_type=MESH).wait_recv()
 
     wide_row = lax.broadcasted_iota(jnp.int32, (ROWS, COLS), 0)
 
@@ -354,13 +375,14 @@
     last = coming[3]
     begin = jnp.clip(last - 2, 0, GROUP - WINDOW)
 
-    def rank(b):
+    def rank(block):
+        b = lax.rem(block + BLOCKS, BLOCKS)
         s = b - 1
         late = jnp.where(s == last, 5, 3)
         for n in (2, 1, 0):
             late = jnp.where(s == coming[n], n + 1, late)
         late = jnp.where(s // NX == zh, 0, late)
-        return jnp.where(jnp.logical_or(b <= 0, b >= BLOCKS - 1), HALO_RANK, late)
+        return jnp.where(b == 0, HALO_RANK, late)
 
     def stage(n):
         def unfold_some(b, carry):
@@ -375,7 +397,7 @@
                 first_step(b)
             return carry
 
-        lax.fori_loop(1, BLOCKS - 1, unfold_some, 0)
+        lax.fori_loop(1, BLOCKS, unfold_some, 0)
         lax.fori_loop(0, BLOCKS, first_some, 0)
 
     def half(n, carry):
@@ -386,33 +408,44 @@
             await_strip(s)
         return carry
 
+    ways = [
+        pltpu.make_async_remote_copy(
+            src_ref=fold.at[way], dst_ref=halo.at[way], send_sem=send_y.at[way], recv_sem=recv_y.at[way],
+            device_id=(px, up if way == 0 else down), device_id_type=MESH)
+        for way in range(2)
+    ]
+    def hand_on(early):
+        for way in range(2):
+            @pl.when((zh + way == 1) == early)
+            def _():
+                pack_rows(way)
+                ways[way].start()
+
     lax.fori_loop(0, NX, half, 0)
+    hand_on(True)
     stage(0)
     await_strip(coming[0])
     stage(1)
     await_strip(coming[1])
+    final[0].start()
+    def take_over():
+        for way in range(2):
+            ways[way].wait()
+        for k in range(KZ + 1):
+            parts = []
+            for way in range(2):
+                turn = (ROWS - 2 * (k % 4) - (2 if way == 0 else 0)) % ROWS
+                part = halo[way, k // 4]
+                parts.append(pltpu.roll(part, turn, 0) if turn else part)
+            pen[k, pl.ds(0, ROWS), :] = jnp.where(wide_row < ROWS // 2, parts[1], parts[0])
+        unfold(0)
+
     stage(2)
     await_strip(coming[2])
-    ways = []
-    for way in range(2):
-        pack_rows(way)
-        copy = pltpu.make_async_remote_copy(
-            src_ref=fold.at[way], dst_ref=halo.at[way], send_sem=send_y.at[way],
-            recv_sem=recv_y.at[way], device_id=(px, up if way == 0 else down), device_id_type=MESH)
-        copy.start()
-        ways.append(copy)
+    hand_on(False)
+    final[1].start()
     stage(3)
-    for way in range(2):
-        ways[way].wait()
-        block = pl.ds(0, ROWS) if way == 0 else pl.ds((GROUP + 1) * ROWS, ROWS)
-        for k in range(KZ + 1):
-            turn = (ROWS - 2 * (k % 4) - (2 if way == 0 else 0)) % ROWS
-            part = halo[way, k // 4]
-            if turn:
-                part = pltpu.roll(part, turn, 0)
-            pen[k, block, :] = part
-    unfold(0)
-    unfold(BLOCKS - 1)
+    take_over()
     stage(HALO_RANK)
 
     def second_come(n, carry):
@@ -421,7 +454,7 @@
         return carry
 
     lax.fori_loop(0, GROUP - WINDOW, second_come, 0)
-    await_strip(last)
+    await_last(last)
     unfold(last + 1)
 
     def first_rest(b, carry):
@@ -454,10 +487,10 @@
             pltpu.VMEM((KZ + 1, BLOCKS * ROWS, COLS), f32),
             pltpu.VMEM((KZ, BLOCKS * ROWS, LANES), f32),
             pltpu.SemaphoreType.DMA((5,)),
-            pltpu.SemaphoreType.DMA((GROUP,)),
+            pltpu.SemaphoreType.DMA((GROUP + 1,)),
             pltpu.SemaphoreType.DMA((3,)),
             pltpu.SemaphoreType.DMA((6,)),
-            pltpu.SemaphoreType.DMA((4,)),
+            pltpu.SemaphoreType.DMA((5,)),
             pltpu.SemaphoreType.DMA((2,)),
             pltpu.SemaphoreType.DMA((2,)),
         ],

time: 71.5 us -> 70.6 us (0.987)
  the two profiles are of different devices: /device:TPU:30 before, /device:TPU:8 now
where the time goes in v3:
time: 70.6 us; the launch traced here: 70.5 us
  Pallas kernels  70.5 us (100%)
    pallas_call x1, Pallas kernels, exchange(): pl.pallas_call(exchange_kernel, out_shape=[pltpu.VMEM((KZ, BLOCKS * ROWS,...  68.8 us
    pallas_call x1, Pallas kernels, finish(): pl.pallas_call(finish_kernel, out_shape=jax.ShapeDtypeStruct(flow.shape,...  1.72 us

profile of v3, /device:TPU:8, one launch (start us, length us, event | category | flops | bytes accessed | tf_op | source)
XLA Modules:
  0.0 70.5 jit_solution(15026367323802617747)
XLA Ops:
  0.0 68.8 %exchange.1 = (f32[38,72,384]{2,1,0:T(8,128)S(1)}, f32[2,72,384]{2,1,0:T(8,128)S(1)}, f32[38,64,256]{2,1,0:T(8,128)S(1)}) custom-call(f32[38,8,2048]{2,1,0:T(8,128)} %bitcast.2, s32[2,8,2048]{2,1,0:T(8,128)} %pore_ref.1), custom_call_target="tpu_custom_call" | custom-call | tf_op jit(solution)/shard_map/exchange/pallas_call | solution.py:470
  68.8 1.7 %finish.1 = f32[38,64,256]{2,1,0:T(8,128)} custom-call(f32[38,72,384]{2,1,0:T(8,128)S(1)} %get-tuple-element.8.post_ref, f32[2,72,384]{2,1,0:T(8,128)S(1)} %get-tuple-element.9.open_ref, f32[38,64,256]{2,1,0:T(8,128)S(1)} %get-tuple-element.10.flow_ref), custom_call_target="tpu_custom_call" | custom-call | tf_op jit(solution)/shard_map/finish/pallas_call | solution.py:531

commit v4 on v3

--- a/solution.py
+++ b/solution.py
@@ -248,17 +248,25 @@
     def piece(p):
         return strip.at[:, :, pl.ds(pl.multiple_of(p * COLS, COLS), COLS)]
 
-    for load in loads[:4]:
-        load.wait()
-    lax.fori_loop(0, 4, early_tile, 0)
+    loads[0].wait()
+    loads[2].wait()
+    lax.fori_loop(1, 3, early_tile, 0)
+    pl.semaphore_wait(barrier, 6)
+
+    opening = [
+        pltpu.make_async_remote_copy(
+            src_ref=piece(partner).at[planes], dst_ref=place(px).at[planes], send_sem=send_z.at[5 * m],
+            recv_sem=give_sem.at[px if m == 0 else GROUP + 1], device_id=(partner, py), device_id_type=MESH)
+        for m, planes in enumerate((pl.ds(0, KZ), pl.ds(KZ, 1)))
+    ]
+    opening[0].start()
+    loads[1].wait()
+    loads[3].wait()
+    early_tile(0, 0)
+    early_tile(3, 0)
     pack_sides(partner)
-    pl.semaphore_wait(barrier, 6)
-
-    first = pltpu.make_async_remote_copy(
-        src_ref=piece(partner), dst_ref=place(px), send_sem=send_z.at[0], recv_sem=give_sem.at[px],
-        device_id=(partner, py), device_id_type=MESH)
-    first.start()
-    sends = [first]
+    opening[1].start()
+    sends = list(opening)
 
     loads[4].wait()
     lax.fori_loop(4, tiles, late_tile, 0)
@@ -316,6 +324,13 @@
         pltpu.make_async_remote_copy(
             src_ref=place(s), dst_ref=place(s), send_sem=send_z.at[0], recv_sem=give_sem.at[s],
             device_id=(partner, py), device_id_type=MESH).wait_recv()
+
+    def await_opening(s):
+        for m, planes in enumerate((pl.ds(0, KZ), pl.ds(KZ, 1))):
+            part = place(s).at[planes]
+            pltpu.make_async_remote_copy(
+                src_ref=part, dst_ref=part, send_sem=send_z.at[0], recv_sem=give_sem.at[s if m == 0 else GROUP + 1],
+                device_id=(partner, py), device_id_type=MESH).wait_recv()
 
     def await_last(s):
         for m, planes in enumerate(halves):
@@ -424,9 +439,15 @@
     lax.fori_loop(0, NX, half, 0)
     hand_on(True)
     stage(0)
-    await_strip(coming[0])
+    await_opening(coming[0])
     stage(1)
     await_strip(coming[1])
+    soon = lax.rem(partner % NX + partner // NX, NX) < 2
+
+    @pl.when(soon)
+    def _():
+        hand_on(False)
+
     final[0].start()
     def take_over():
         for way in range(2):
@@ -442,7 +463,11 @@
 
     stage(2)
     await_strip(coming[2])
-    hand_on(False)
+
+    @pl.when(jnp.logical_not(soon))
+    def _():
+        hand_on(False)
+
     final[1].start()
     stage(3)
     take_over()
@@ -487,10 +512,10 @@
             pltpu.VMEM((KZ + 1, BLOCKS * ROWS, COLS), f32),
             pltpu.VMEM((KZ, BLOCKS * ROWS, LANES), f32),
             pltpu.SemaphoreType.DMA((5,)),
-            pltpu.SemaphoreType.DMA((GROUP + 1,)),
+            pltpu.SemaphoreType.DMA((GROUP + 2,)),
             pltpu.SemaphoreType.DMA((3,)),
             pltpu.SemaphoreType.DMA((6,)),
-            pltpu.SemaphoreType.DMA((5,)),
+            pltpu.SemaphoreType.DMA((6,)),
             pltpu.SemaphoreType.DMA((2,)),
             pltpu.SemaphoreType.DMA((2,)),
         ],

time: 70.6 us -> 70.6 us (level)
  no operation moved by 1% of the time
where the time goes in v4:
time: 70.6 us; the launch traced here: 70.5 us
  Pallas kernels  70.5 us (100%)
    pallas_call x1, Pallas kernels, exchange(): pl.pallas_call(exchange_kernel, out_shape=[pltpu.VMEM((KZ, BLOCKS * ROWS,...  68.8 us
    pallas_call x1, Pallas kernels, finish(): pl.pallas_call(finish_kernel, out_shape=jax.ShapeDtypeStruct(flow.shape,...  1.72 us

profile of v4, /device:TPU:8, one launch (start us, length us, event | category | flops | bytes accessed | tf_op | source)
XLA Modules:
  0.0 70.5 jit_solution(2180660543838428284)
XLA Ops:
  0.0 68.8 %exchange.1 = (f32[38,72,384]{2,1,0:T(8,128)S(1)}, f32[2,72,384]{2,1,0:T(8,128)S(1)}, f32[38,64,256]{2,1,0:T(8,128)S(1)}) custom-call(f32[38,8,2048]{2,1,0:T(8,128)} %bitcast.2, s32[2,8,2048]{2,1,0:T(8,128)} %pore_ref.1), custom_call_target="tpu_custom_call" | custom-call | tf_op jit(solution)/shard_map/exchange/pallas_call | solution.py:495
  68.8 1.7 %finish.1 = f32[38,64,256]{2,1,0:T(8,128)} custom-call(f32[38,72,384]{2,1,0:T(8,128)S(1)} %get-tuple-element.8.post_ref, f32[2,72,384]{2,1,0:T(8,128)S(1)} %get-tuple-element.9.open_ref, f32[38,64,256]{2,1,0:T(8,128)S(1)} %get-tuple-element.10.flow_ref), custom_call_target="tpu_custom_call" | custom-call | tf_op jit(solution)/shard_map/finish/pallas_call | solution.py:556
